TPU v7x, 32 devices: a whole 2x2x4 slice. The times are simulated.
32 devices in a mesh: dp: 8 (over z, core), tensor: 4 (over y, x).
Axes of the slice: x: 2, y: 2, z: 4, core: 2. Of those that a mesh axis runs over, the one named last changes fastest.
Arguments:
- prompt_ids: int32 [4096], P(('dp', 'tensor')), may hold values from 0 to 128255
- prompt_lengths: int32 [8], replicated, may hold values from 1 to 512, as said below
- embed_table: bfloat16 [4096, 128256], P(('dp', 'tensor')), may hold values from -4 to 4
- norm_gain: float32 [4096], replicated, may hold values from 0.5 to 1.5
- w_query: bfloat16 [4096, 4096], P('dp', 'tensor'), may hold values from -3 to 3
- w_key: bfloat16 [4096, 1024], P('dp', 'tensor'), may hold values from -1 to 1
- w_value: bfloat16 [4096, 1024], P('dp', 'tensor'), may hold values from -0.09375 to 0.09375
- w_out: bfloat16 [4096, 4096], P('tensor', 'dp'), may hold values from -0.09375 to 0.09375
Outputs:
- hidden: bfloat16 [4096, 4096], P(('dp', 'tensor'))
- kv_cache: bfloat16 [32, 2, 512, 256], P(('dp', 'tensor'))
Inputs may be any that keep to these rules, and one draw needn't show every extreme that they name: `prompt_lengths`: each group's prompt has 1 to 512 live tokens, and some group's has 512.
All inputs are finite; a program needn't handle non-finite values.
Results may differ from a plain program's by a relative error of at most 0.0095.
Values may be sent and summed in bfloat16 or wider, within the bound.
A program may use at most 192 MiB of HBM per device.

v0:
```python
import jax
import jax.numpy as jnp
from jax import lax
from jax.sharding import PartitionSpec as P

HEADS = 32
KVH = 8
HD = 128
TPG = 4
norm_eps = 1e-05
rope_theta = 500000.0


def swapped(block, axis, apart):
    count = lax.axis_size(axis)
    route = []
    for low in range(count):
        high = low | 1 << apart
        if high != low and high < count:
            route += [(low, high), (high, low)]
    return lax.ppermute(block, axis, route)


def for_sending(shard):

    def short(part):
        return part.astype(jnp.bfloat16) if part.dtype == jnp.float32 else part

    return jax.tree.map(short, shard)


def rotate(heads_in, positions):
    half = heads_in.shape[-1] // 2
    freq = rope_theta ** (-2.0 * jnp.arange(half, dtype=jnp.float32) / heads_in.shape[-1])
    angle = positions.astype(jnp.float32)[:, None] * freq[None, :]
    cosine = jnp.cos(angle)[:, None, :]
    sine = jnp.sin(angle)[:, None, :]
    first = heads_in[..., :half]
    second = heads_in[..., half:]
    return jnp.concatenate(
        [first * cosine - second * sine, second * cosine + first * sine], axis=-1
    )


def attend(query_rot, key_rot, value_rows, length):
    row_count = query_rot.shape[0]
    block = min(512, row_count)
    positions = jnp.arange(row_count, dtype=jnp.int32)

    def one_block(offset):
        scores = jnp.einsum(
            "qhgd,khd->hgqk", query_rot, key_rot, preferred_element_type=jnp.float32
        ) / jnp.sqrt(jnp.float32(HD))
        query_pos = offset + jnp.arange(block, dtype=jnp.int32)
        allowed = (positions[None, :] <= query_pos[:, None]) & (positions[None, :] < length)
        scores = jnp.where(allowed, scores, -1e30)
        biggest = jnp.max(scores, axis=-1, keepdims=True)
        expd = jnp.exp(scores - biggest)
        weights = (expd / jnp.sum(expd, axis=-1, keepdims=True)).astype(jnp.bfloat16)
        result = jnp.einsum(
            "hgqk,khd->qhgd", weights, value_rows, preferred_element_type=jnp.float32
        )
        return result.astype(jnp.bfloat16)

    starts = jnp.arange(0, row_count, block, dtype=jnp.int32)
    outs = lax.map(one_block, starts)
    return outs.reshape(row_count, -1)


def ordered_pair(mine, theirs, bit_index):
    upper_half = lax.axis_index("tensor") >> bit_index & 1 == 1
    first_half = jnp.where(upper_half, theirs, mine)
    second_half = jnp.where(upper_half, mine, theirs)
    return jnp.concatenate([first_half, second_half], axis=0)


def collect_blocks(shard, swapper):
    stacked = shard[None]
    levels = lax.axis_size("tensor").bit_length() - 1
    for bit_index in range(TPG.bit_length() - 1, levels):
        stacked = ordered_pair(stacked, swapper(stacked, bit_index), bit_index)
    return stacked


def gather_in_group(own_part):
    joined = own_part
    for bit_index in range(TPG.bit_length() - 1):
        joined = ordered_pair(joined, swapped(joined, "tensor", bit_index), bit_index)
    return joined


def rms_normed(tokens_in, norm_gain):
    wide_in = tokens_in.astype(jnp.float32)
    scale = lax.rsqrt(jnp.mean(wide_in * wide_in, axis=1, keepdims=True) + norm_eps)
    return (wide_in * scale * norm_gain[None, :]).astype(jnp.bfloat16)


def lookup_rows(embed_table, token_ids):
    columns = embed_table.shape[0]
    vocab_size = embed_table.shape[1]
    packing = max(1, 128 // columns)
    token_major = embed_table.T.reshape(vocab_size // packing, packing * columns)
    fetched = jnp.take(token_major, token_ids // packing, axis=0).reshape(
        token_ids.shape[0], packing, columns
    )
    if packing == 1:
        return fetched.reshape(token_ids.shape[0], columns)
    slot_ids = jnp.arange(packing, dtype=jnp.int32)
    wanted = (token_ids % packing)[:, None] == slot_ids[None, :]
    chosen = jnp.where(wanted[:, :, None], fetched, jnp.zeros_like(fetched))
    return jnp.sum(chosen, axis=1, dtype=jnp.bfloat16)


def shards(prompt_ids, prompt_lengths, embed_table, norm_gain, w_query, w_key, w_value, w_out):
    quarter = prompt_ids.shape[0]
    row_count = quarter * TPG
    devices = lax.axis_size(("dp", "tensor"))
    columns = embed_table.shape[0]
    model_width = columns * devices
    group_index = (
        lax.axis_index("dp") * (lax.axis_size("tensor") // TPG) + lax.axis_index("tensor") // TPG
    )
    length = lax.dynamic_slice_in_dim(prompt_lengths, group_index, 1, 0)[0]
    all_ids = lax.all_gather(prompt_ids, ("dp", "tensor"), axis=0, tiled=True)
    picked = lookup_rows(embed_table, all_ids)
    outgoing = picked.reshape(devices, quarter, columns)
    arrived = lax.all_to_all(outgoing, ("dp", "tensor"), split_axis=0, concat_axis=2, tiled=True)
    own_rows = arrived.reshape(quarter, model_width)
    normed = gather_in_group(rms_normed(own_rows, norm_gain))
    query_width = w_query.shape[1]
    key_width = w_key.shape[1]
    packed = jnp.concatenate([w_query, w_key, w_value], axis=1)
    stacked = collect_blocks(
        packed,
        lambda values, bit_index: jax.tree.map(
            lambda part, own: part.astype(own.dtype),
            swapped(for_sending(values), "tensor", bit_index),
            values,
        ),
    )
    projected = jnp.einsum(
        "rd,kdc->rkc",
        normed,
        lax.all_gather(stacked, "dp", axis=1, tiled=True),
        preferred_element_type=jnp.float32,
    )
    blocks = projected.shape[1]
    local_heads = blocks * query_width // HD
    local_kv = blocks * key_width // HD
    positions = jnp.arange(row_count, dtype=jnp.int32)
    query = projected[:, :, :query_width].reshape(row_count, local_heads, HD)
    key_raw = projected[:, :, query_width : query_width + key_width].reshape(
        row_count, local_kv, HD
    )
    value_raw = projected[:, :, query_width + key_width :].reshape(row_count, local_kv, HD)
    query_rot = rotate(query, positions).astype(jnp.bfloat16)
    key_rot = rotate(key_raw, positions).astype(jnp.bfloat16)
    value_rows = value_raw.astype(jnp.bfloat16)
    cache = jnp.stack(
        [key_rot.reshape(row_count, local_kv * HD), value_rows.reshape(row_count, local_kv * HD)],
        axis=0,
    )[None]
    attended = attend(
        query_rot.reshape(row_count, local_kv, HEADS // KVH, HD), key_rot, value_rows, length
    )
    attended = attended.reshape(row_count, blocks, query_width)
    out_blocks = collect_blocks(
        w_out,
        lambda values, bit_index: jax.tree.map(
            lambda part, own: part.astype(own.dtype),
            swapped(for_sending(values), "tensor", bit_index),
            values,
        ),
    )
    partial_sum = jnp.einsum(
        "rkw,kwc->rc",
        attended,
        lax.all_gather(out_blocks, "dp", axis=2, tiled=True),
        preferred_element_type=jnp.float32,
    )
    levels_in = TPG.bit_length() - 1
    running = partial_sum
    for bit_index in reversed(range(levels_in)):
        half_rows = running.shape[0] // 2
        upper_half = lax.axis_index("tensor") >> bit_index & 1 == 1
        kept = jnp.where(upper_half, running[half_rows:], running[:half_rows]).astype(jnp.bfloat16)
        given = jnp.where(upper_half, running[:half_rows], running[half_rows:]).astype(jnp.bfloat16)
        arrived_sum = swapped(given, "tensor", bit_index)
        running = kept.astype(jnp.float32) + arrived_sum.astype(jnp.float32)
    hidden = (own_rows.astype(jnp.float32) + running).astype(jnp.bfloat16)
    return (hidden, cache)


def solution(mesh):
    in_specs = (
        P(("dp", "tensor")),
        P(),
        P(("dp", "tensor"), None),
        P(),
        P("dp", "tensor"),
        P("dp", "tensor"),
        P("dp", "tensor"),
        P("tensor", "dp"),
    )
    out_specs = (P(("dp", "tensor"), None), P(("dp", "tensor"), None, None, None))
    return jax.shard_map(shards, mesh=mesh, in_specs=in_specs, out_specs=out_specs, check_vma=False)
```

profile of v0, /device:TPU:28, one launch (start us, length us, event | category | flops | bytes accessed | tf_op | source)
XLA Modules:
  0.0 427.4 jit_solution(1103278415025191674)
XLA Ops:
  7.2 2.7 pad_maximum_fusion.1
  9.9 42.6 %copy.29 = bf16[128,128256]{0,1:T(8,128)(2,1)} copy(bf16[128,128256]{1,0:T(8,128)(2,1)} %param.10) | data formatting | bytes 65667072 | tf_op args[2]
  52.6 61.9 %all-gather.2 = s32[32,1,128]{2,1,0:T(1,128)S(1)} all-gather(s32[1,1,128]{2,1,0:T(1,128)S(1)} %bitcast.78), channel_id=1, replica_groups=mesh['dp'=8,'tensor'=4] {'dp','tensor'}, dimensions={0}, use_global_device_ids=true | all-gather | bytes 16896 | tf_op jit(solution)/shard_map/all_gather | solution.py:124
  114.5 43.0 %gather_fusion = bf16[4096,128]{1,0:T(8,128)(2,1)S(1)} fusion(bf16[128256,128]{1,0:T(8,128)(2,1)} %bitcast.67, s32[4096]{0:T(1024)S(1)} %fusion.24), kind=kCustom, calls=%fused_computation | custom fusion | bytes 2113536 | tf_op jit(solution)/shard_map/jit(_take)/gather | solution.py:103
  157.5 1.5 broadcast_select_fusion.4
  159.0 12.5 %all-to-all-start = ((bf16[32,128,128]{2,1,0:T(8,128)(2,1)}), bf16[32,128,128]{2,1,0:T(8,128)(2,1)S(1)}, u32[]{:S(2)}, u32[]{:S(2)}) async-start(bf16[32,128,128]{2,1,0:T(8,128)(2,1)} %broadcast_select_fusion.4), calls=%async_computation | async-start | bytes 2097152 | tf_op jit(solution)/shard_map/all_to_all | solution.py:127
  172.3 44.7 %all-to-all-done = bf16[32,128,128]{2,1,0:T(8,128)(2,1)S(1)} async-done(((bf16[32,128,128]{2,1,0:T(8,128)(2,1)}), bf16[32,128,128]{2,1,0:T(8,128)(2,1)S(1)}, u32[]{:S(2)}, u32[]{:S(2)}) %all-to-all-start) | async-done | bytes 1048608 | tf_op jit(solution)/shard_map/all_to_all | solution.py:127
  217.2 1.2 copy.30
  218.8 1.8 fusion.15
  220.6 1.2 collective-permute-start
  221.8 24.0 %collective-permute-done = bf16[128,4096]{1,0:T(8,128)(2,1)} collective-permute-done((bf16[128,4096]{1,0:T(8,128)(2,1)S(1)}, bf16[128,4096]{1,0:T(8,128)(2,1)}, u32[]{:S(2)}, u32[]{:S(2)}) %collective-permute-start) | collective-permute-done | bytes 1048608 | tf_op jit(solution)/shard_map/ppermute | solution.py:21
  245.8 3.0 broadcast_select_fusion.3
  248.9 1.7 pad_maximum_fusion
  252.9 1.7 multiply_cosine_fusion
  254.6 42.9 %collective-permute-done.1 = bf16[256,4096]{1,0:T(8,128)(2,1)} collective-permute-done((bf16[256,4096]{1,0:T(8,128)(2,1)}, bf16[256,4096]{1,0:T(8,128)(2,1)}, u32[]{:S(2)}, u32[]{:S(2)}) %collective-permute-start.1) | collective-permute-done | bytes 2097184 | tf_op jit(solution)/shard_map/ppermute | solution.py:21
  297.5 5.1 %broadcast_select_fusion.1 = (bf16[256,4096]{1,0:T(8,128)(2,1)}, bf16[256,4096]{1,0:T(8,128)(2,1)}) fusion(bf16[256,4096]{1,0:T(8,128)(2,1)} %collective-permute-done.1, pred[]{:T(512)S(6)} %eq.9, bf16[128,4096]{1,0:T(8,128)(2,1)} %copy-done.1, bf16[128,4096]{1,0:T(8,128)(2,1)S(1)} %get-tuple-element.20), kind=kLoop, calls=%fused_computation.33 | loop fusion | flops 6291456 | bytes 8388609 | tf_op jit(solution)/shard_map/jit(_where)/select_n | solution.py:72
  302.6 10.6 %fusion.10 = f32[512,1,1536]{2,0,1:T(8,128)S(1)} fusion(bf16[4096,1536]{1,0:T(8,128)(2,1)} %all-gather.6.cloned.1.call-done, bf16[256,4096]{1,0:T(8,128)(2,1)} %get-tuple-element.17, bf16[256,4096]{1,0:T(8,128)(2,1)} %get-tuple-element.16), kind=kOutput, calls=%fused_computation.17 | convolution fusion | flops 6450839552 | bytes 19922944 | tf_op jit(solution)/shard_map/rd,kdc->rkc/dot_general | solution.py:141
  313.2 1.6 copy-done.4
  315.8 1.7 slice_bitcast_fusion
  319.4 1.2 copy.33
  320.6 1.1 copy.34
  324.2 1.3 fusion.18
  325.5 5.6 %fusion.30 = (f32[2,4,512]{2,1,0:T(4,128)S(1)}, f32[2,4,512,512]{2,3,1,0:T(8,128)}) fusion(f32[2,512,512,4]{2,1,3,0:T(8,128)S(1)} %fusion.18, pred[512,512]{0,1:T(8,128)(4,1)S(1)} %copy-done.7), kind=kOutput, calls=%fused_computation.65 | output fusion | flops 12583423 | bytes 17055744 | tf_op jit(solution)/shard_map/while/body/eval_jaxpr/sub | solution.py:58
  331.2 4.1 fusion.17
  335.3 8.4 %fusion.31 = bf16[512,4096]{1,0:T(8,128)(2,1)S(1)} fusion(bf16[512,1024]{0,1:T(8,128)(2,1)S(1)} %bitcast.79, bf16[1024,4096]{1,0:T(8,128)(2,1)} %all-gather.8.cloned.1.call-done), kind=kOutput, calls=%fused_computation.67 | convolution fusion | flops 4294967296 | bytes 13631488 | tf_op jit(solution)/shard_map/rkw,kwc->rc/dot_general | solution.py:175
  344.3 45.5 %collective-permute-done.2 = bf16[256,4096]{1,0:T(8,128)(2,1)S(1)} collective-permute-done((bf16[256,4096]{1,0:T(8,128)(2,1)S(1)}, bf16[256,4096]{1,0:T(8,128)(2,1)S(1)}, u32[]{:S(2)}, u32[]{:S(2)}) %collective-permute-start.2) | collective-permute-done | bytes 2097184 | tf_op jit(solution)/shard_map/ppermute | solution.py:21
  389.9 1.2 convert_add_fusion
  391.1 1.3 copy-done
  392.4 1.1 select_convert_fusion.2
  395.6 1.1 convert_element_type.134
  398.6 17.6 %collective-permute-done.3 = bf16[128,4096]{1,0:T(8,128)(2,1)S(1)} collective-permute-done((bf16[128,4096]{1,0:T(8,128)(2,1)}, bf16[128,4096]{1,0:T(8,128)(2,1)S(1)}, u32[]{:S(2)}, u32[]{:S(2)}) %collective-permute-start.3) | collective-permute-done | bytes 1048608 | tf_op jit(solution)/shard_map/ppermute | solution.py:21
  416.2 4.3 %fusion.16 = bf16[128,4096]{1,0:T(8,128)(2,1)} fusion(bf16[128,4096]{1,0:T(8,128)(2,1)S(1)} %collective-permute-done.3, f32[16,8,32,128]{3,2,1,0:T(8,128)S(1)} %bitcast.70, bf16[256,4096]{1,0:T(8,128)(2,1)} %copy-done, pred[]{:T(512)S(6)} %eq.8), kind=kLoop, calls=%fused_computation.25 | loop fusion | flops 3145728 | bytes 6291457 | tf_op jit(solution)/shard_map/convert_element_type | solution.py:190
  (54 shorter events, 13.5 us)
Async XLA Ops:
  7.2 295.4 %all-gather.6.cloned.1.call-start = ((), (), s32[]{:S(2)}) async-start(), calls=%async_computation.1 | async-start | bytes 14155776 | tf_op jit(solution)/shard_map/all_gather | solution.py:144
  9.9 42.7 %copy-start.10 = (s32[128]{0:T(128)S(1)}, s32[128]{0:T(128)}, u32[]{:S(2)}) copy-start(s32[128]{0:T(128)} %param.8) | copy-start | bytes 1540
  159.0 57.9 %all-to-all-start = ((bf16[32,128,128]{2,1,0:T(8,128)(2,1)}), bf16[32,128,128]{2,1,0:T(8,128)(2,1)S(1)}, u32[]{:S(2)}, u32[]{:S(2)}) async-start(bf16[32,128,128]{2,1,0:T(8,128)(2,1)} %broadcast_select_fusion.4), calls=%async_computation | async-start | bytes 2097152 | tf_op jit(solution)/shard_map/all_to_all | solution.py:127
  171.5 163.8 %all-gather.8.cloned.1.call-start = ((), (), s32[]{:S(2)}) async-start(), calls=%async_computation.2 | async-start | bytes 9437184 | tf_op jit(solution)/shard_map/all_gather | solution.py:178
  217.2 1.5 copy-start.9
  220.6 25.2 %collective-permute-start = (bf16[128,4096]{1,0:T(8,128)(2,1)S(1)}, bf16[128,4096]{1,0:T(8,128)(2,1)}, u32[]{:S(2)}, u32[]{:S(2)}) collective-permute-start(bf16[128,4096]{1,0:T(8,128)(2,1)S(1)} %fusion.15), channel_id=1, source_target_pairs={{0,1},{1,0},{2,3},{3,2},{4,5},{5,4},{6,7},{7,6},{8,9},{9,8},{10,11... | collective-permute-start | bytes 3145736 | tf_op jit(solution)/shard_map/ppermute | solution.py:21
  248.8 1.7 copy-start.1
  248.8 1.9 copy-start.11
  250.5 47.0 %collective-permute-start.1 = (bf16[256,4096]{1,0:T(8,128)(2,1)}, bf16[256,4096]{1,0:T(8,128)(2,1)}, u32[]{:S(2)}, u32[]{:S(2)}) collective-permute-start(bf16[256,4096]{1,0:T(8,128)(2,1)} %pad_maximum_fusion), channel_id=1, source_target_pairs={{0,2},{2,0},{1,3},{3,1},{4,6},{6,4},{5,7},{7,5},{8,10},{10,8},{9,1... | collective-permute-start | bytes 6291464 | tf_op jit(solution)/shard_map/ppermute | solution.py:21
  313.2 1.6 copy-start.4
  317.6 1.0 copy-start.5
  319.4 2.4 copy-start.6
  322.6 1.2 copy-start.2
  322.6 1.5 copy-start.3
  324.2 1.4 copy-start.7
  325.5 5.7 %copy-start.8 = (bf16[512,1,256]{0,2,1:T(8,128)(2,1)S(1)}, bf16[512,1,256]{0,2,1:T(8,128)(2,1)}, u32[]{:S(2)}) copy-start(bf16[512,1,256]{0,2,1:T(8,128)(2,1)} %copy.41) | copy-start | bytes 786436
  344.0 45.9 %collective-permute-start.2 = (bf16[256,4096]{1,0:T(8,128)(2,1)S(1)}, bf16[256,4096]{1,0:T(8,128)(2,1)S(1)}, u32[]{:S(2)}, u32[]{:S(2)}) collective-permute-start(bf16[256,4096]{1,0:T(8,128)(2,1)S(1)} %select_convert_fusion), channel_id=1, source_target_pairs={{0,2},{2,0},{1,3},{3,1},{4,6},{6,4},{5,7},{7,5},{8,10},{10,8},{9,1... | collective-permute-start | bytes 6291464 | tf_op jit(solution)/shard_map/ppermute | solution.py:21
  391.1 1.3 copy-start
  393.5 22.7 %collective-permute-start.3 = (bf16[128,4096]{1,0:T(8,128)(2,1)}, bf16[128,4096]{1,0:T(8,128)(2,1)S(1)}, u32[]{:S(2)}, u32[]{:S(2)}) collective-permute-start(bf16[128,4096]{1,0:T(8,128)(2,1)} %select_convert_fusion.2), channel_id=1, source_target_pairs={{0,1},{1,0},{2,3},{3,2},{4,5},{5,4},{6,7},{7,6},{8,9},{9,8},{10,11... | collective-permute-start | bytes 3145736 | tf_op jit(solution)/shard_map/ppermute | solution.py:21
Sparse Core Ops, SparseCore 0:
  10.0 114.7 all-gather.5
  173.9 90.8 all-gather.7
where the time goes:
time: 429 us; the launch traced here: 427 us
  waiting for transfers between devices  175 us (41%)
  local copies, waits for them, and re-layouts  102 us (24%)
  blocking collectives  61.9 us (14%)
  other arithmetic  34 us (8%)
  matrix products  24.5 us (6%)
  starting transfers between devices  15.5 us (4%)
  between operations  14.3 us (3%)
    ppermute x4, waiting for transfers between devices, swapped(): return lax.ppermute(block, axis, route)  130 us
    all_gather x1, blocking collectives, shards(): all_ids = lax.all_gather(prompt_ids, ('dp', 'tensor'), axis=0, tiled=True)  61.9 us
    unnamed x27, local copies, waits for them, and re-layouts  48.9 us
    all_to_all x1, waiting for transfers between devices, shards(): lax.all_to_all(outgoing, ('dp', 'tensor'), split_axis=0, concat_axis=2, t...  44.7 us
    gather x1, local copies, waits for them, and re-layouts, lookup_rows(): jnp.take(token_major, token_ids // packing, axis=0)  43 us
    all_to_all x1, starting transfers between devices, shards(): lax.all_to_all(outgoing, ('dp', 'tensor'), split_axis=0, concat_axis=2, t...  12.5 us
    dot_general x1, matrix products, shards(): jnp.einsum('rd,kdc->rkc', normed, lax.all_gather(stacked, 'dp', axis=1, t...  10.6 us
  transfers between devices with their start and end apart: 7, of which 5 were waited for; matrix products, arithmetic and copies ran while one was open for 32% of the time, Pallas kernels for 0%

commit v1 on v0

--- a/solution.py
+++ b/solution.py
@@ -124,7 +124,15 @@
     all_ids = lax.all_gather(prompt_ids, ("dp", "tensor"), axis=0, tiled=True)
     picked = lookup_rows(embed_table, all_ids)
     outgoing = picked.reshape(devices, quarter, columns)
-    arrived = lax.all_to_all(outgoing, ("dp", "tensor"), split_axis=0, concat_axis=2, tiled=True)
+    arrived = jnp.concatenate(
+        lax.all_to_all(
+            jnp.stack(jnp.split(outgoing, lax.axis_size(("dp", "tensor")), axis=0)),
+            ("dp", "tensor"),
+            0,
+            0,
+        ),
+        axis=2,
+    )
     own_rows = arrived.reshape(quarter, model_width)
     normed = gather_in_group(rms_normed(own_rows, norm_gain))
     query_width = w_query.shape[1]

time: 429 us -> 450 us (1.049)
  local copies, waits for them, and re-layouts: 102 us -> 121 us
    unnamed x27 -> x58, local copies, waits for them, and re-layouts: 48.9 us -> 68 us
  transfers between devices with their start and end apart: 7 -> 7, of which waited for: 5 -> 5; matrix products, arithmetic and copies ran while one was open for 32% -> 35% of each run, Pallas kernels for 0% -> 0%
where the time goes in v1:
time: 450 us; the launch traced here: 448 us
  waiting for transfers between devices  176 us (39%)
  local copies, waits for them, and re-layouts  121 us (27%)
  blocking collectives  61.9 us (14%)
  other arithmetic  34.7 us (8%)
  matrix products  24.5 us (5%)
  starting transfers between devices  15.4 us (3%)
  between operations  14.3 us (3%)
    ppermute x4, waiting for transfers between devices, swapped(): return lax.ppermute(block, axis, route)  130 us
    unnamed x58, local copies, waits for them, and re-layouts  68 us
    all_gather x1, blocking collectives, shards(): all_ids = lax.all_gather(prompt_ids, ('dp', 'tensor'), axis=0, tiled=True)  61.9 us
    all_to_all x1, waiting for transfers between devices, shards(): lax.all_to_all(jnp.stack(jnp.split(outgoing, lax.axis_size(('dp', 'tensor...  44.7 us
    gather x1, local copies, waits for them, and re-layouts, lookup_rows(): jnp.take(token_major, token_ids // packing, axis=0)  43 us
    all_to_all x1, starting transfers between devices, shards(): lax.all_to_all(jnp.stack(jnp.split(outgoing, lax.axis_size(('dp', 'tensor...  12.5 us
    dot_general x1, matrix products, shards(): jnp.einsum('rd,kdc->rkc', normed, lax.all_gather(stacked, 'dp', axis=1, t...  10.6 us
  transfers between devices with their start and end apart: 7, of which 5 were waited for; matrix products, arithmetic and copies ran while one was open for 35% of the time, Pallas kernels for 0%

profile of v1, /device:TPU:28, one launch (start us, length us, event | category | flops | bytes accessed | tf_op | source)
XLA Modules:
  0.0 447.8 jit_solution(745390748643489515)
XLA Ops:
  7.2 2.7 pad_maximum_fusion.1
  9.9 42.6 %copy.19 = bf16[128,128256]{0,1:T(8,128)(2,1)} copy(bf16[128,128256]{1,0:T(8,128)(2,1)} %param.10) | data formatting | bytes 65667072 | tf_op args[2]
  52.6 61.9 %all-gather.2 = s32[32,1,128]{2,1,0:T(1,128)S(1)} all-gather(s32[1,1,128]{2,1,0:T(1,128)S(1)} %bitcast.200), channel_id=1, replica_groups=mesh['dp'=8,'tensor'=4] {'dp','tensor'}, dimensions={0}, use_global_device_ids=true | all-gather | bytes 16896 | tf_op jit(solution)/shard_map/all_gather | solution.py:124
  114.5 43.0 %gather_fusion = bf16[4096,128]{1,0:T(8,128)(2,1)S(1)} fusion(bf16[128256,128]{1,0:T(8,128)(2,1)} %bitcast.190, s32[4096]{0:T(1024)S(1)} %fusion.24), kind=kCustom, calls=%fused_computation | custom fusion | bytes 2113536 | tf_op jit(solution)/shard_map/jit(_take)/gather | solution.py:103
  157.5 2.1 broadcast_select_fusion.2
  179.5 12.5 %all-to-all-start = ((bf16[32,1,128,128]{3,2,1,0:T(8,128)(2,1)}), bf16[32,1,128,128]{3,2,1,0:T(8,128)(2,1)S(1)}, u32[]{:S(2)}, u32[]{:S(2)}) async-start(bf16[32,1,128,128]{3,2,1,0:T(8,128)(2,1)} %constant_dynamic-update-slice_fusion), calls=%async_computation | async-start | bytes 2097152 | tf_op jit(solution)/shard_map/all_to_all | solution.py:128
  192.7 44.7 %all-to-all-done = bf16[32,1,128,128]{3,2,1,0:T(8,128)(2,1)S(1)} async-done(((bf16[32,1,128,128]{3,2,1,0:T(8,128)(2,1)}), bf16[32,1,128,128]{3,2,1,0:T(8,128)(2,1)S(1)}, u32[]{:S(2)}, u32[]{:S(2)}) %all-to-all-start) | async-done | bytes 1048608 | tf_op jit(solution)/shard_map/all_to_all | solution.py:128
  237.6 1.2 copy.20
  239.2 1.8 fusion.15
  241.0 1.2 collective-permute-start
  242.3 24.0 %collective-permute-done = bf16[128,4096]{1,0:T(8,128)(2,1)} collective-permute-done((bf16[128,4096]{1,0:T(8,128)(2,1)S(1)}, bf16[128,4096]{1,0:T(8,128)(2,1)}, u32[]{:S(2)}, u32[]{:S(2)}) %collective-permute-start) | collective-permute-done | bytes 1048608 | tf_op jit(solution)/shard_map/ppermute | solution.py:21
  266.3 3.0 broadcast_select_fusion.4
  269.3 1.7 pad_maximum_fusion
  273.3 1.7 multiply_cosine_fusion
  275.0 42.9 %collective-permute-done.1 = bf16[256,4096]{1,0:T(8,128)(2,1)} collective-permute-done((bf16[256,4096]{1,0:T(8,128)(2,1)}, bf16[256,4096]{1,0:T(8,128)(2,1)}, u32[]{:S(2)}, u32[]{:S(2)}) %collective-permute-start.1) | collective-permute-done | bytes 2097184 | tf_op jit(solution)/shard_map/ppermute | solution.py:21
  317.9 5.1 %broadcast_select_fusion.1 = (bf16[256,4096]{1,0:T(8,128)(2,1)}, bf16[256,4096]{1,0:T(8,128)(2,1)}) fusion(bf16[256,4096]{1,0:T(8,128)(2,1)} %collective-permute-done.1, pred[]{:T(512)S(6)} %eq.9, bf16[128,4096]{1,0:T(8,128)(2,1)} %copy-done.1, bf16[128,4096]{1,0:T(8,128)(2,1)S(1)} %get-tuple-element.20), kind=kLoop, calls=%fused_computation.33 | loop fusion | flops 6291456 | bytes 8388609 | tf_op jit(solution)/shard_map/jit(_where)/select_n | solution.py:72
  323.0 10.6 %fusion.10 = f32[512,1,1536]{2,0,1:T(8,128)S(1)} fusion(bf16[4096,1536]{1,0:T(8,128)(2,1)} %all-gather.6.cloned.1.call-done, bf16[256,4096]{1,0:T(8,128)(2,1)} %get-tuple-element.17, bf16[256,4096]{1,0:T(8,128)(2,1)} %get-tuple-element.16), kind=kOutput, calls=%fused_computation.17 | convolution fusion | flops 6450839552 | bytes 19922944 | tf_op jit(solution)/shard_map/rd,kdc->rkc/dot_general | solution.py:149
  333.7 1.6 copy-done.4
  336.3 1.7 slice_bitcast_fusion
  339.8 1.2 copy.23
  341.0 1.1 copy.24
  344.6 1.3 fusion.18
  345.9 5.6 %fusion.30 = (f32[2,4,512]{2,1,0:T(4,128)S(1)}, f32[2,4,512,512]{2,3,1,0:T(8,128)}) fusion(f32[2,512,512,4]{2,1,3,0:T(8,128)S(1)} %fusion.18, pred[512,512]{0,1:T(8,128)(4,1)S(1)} %copy-done.7), kind=kOutput, calls=%fused_computation.129 | output fusion | flops 12583423 | bytes 17055744 | tf_op jit(solution)/shard_map/while/body/eval_jaxpr/sub | solution.py:58
  351.6 4.1 fusion.17
  355.7 8.4 %fusion.31 = bf16[512,4096]{1,0:T(8,128)(2,1)S(1)} fusion(bf16[512,1024]{0,1:T(8,128)(2,1)S(1)} %bitcast.201, bf16[1024,4096]{1,0:T(8,128)(2,1)} %all-gather.8.cloned.1.call-done), kind=kOutput, calls=%fused_computation.131 | convolution fusion | flops 4294967296 | bytes 13631488 | tf_op jit(solution)/shard_map/rkw,kwc->rc/dot_general | solution.py:183
  364.7 45.6 %collective-permute-done.2 = bf16[256,4096]{1,0:T(8,128)(2,1)S(1)} collective-permute-done((bf16[256,4096]{1,0:T(8,128)(2,1)S(1)}, bf16[256,4096]{1,0:T(8,128)(2,1)S(1)}, u32[]{:S(2)}, u32[]{:S(2)}) %collective-permute-start.2) | collective-permute-done | bytes 2097184 | tf_op jit(solution)/shard_map/ppermute | solution.py:21
  410.3 1.2 convert_add_fusion
  411.5 1.3 copy-done
  412.9 1.1 select_convert_fusion.2
  415.9 1.1 convert_element_type.129
  419.0 17.7 %collective-permute-done.3 = bf16[128,4096]{1,0:T(8,128)(2,1)S(1)} collective-permute-done((bf16[128,4096]{1,0:T(8,128)(2,1)}, bf16[128,4096]{1,0:T(8,128)(2,1)S(1)}, u32[]{:S(2)}, u32[]{:S(2)}) %collective-permute-start.3) | collective-permute-done | bytes 1048608 | tf_op jit(solution)/shard_map/ppermute | solution.py:21
  436.7 4.3 fusion.16
  (86 shorter events, 33.1 us)
Async XLA Ops:
  7.2 315.8 %all-gather.6.cloned.1.call-start = ((), (), s32[]{:S(2)}) async-start(), calls=%async_computation.1 | async-start | bytes 14155776 | tf_op jit(solution)/shard_map/all_gather | solution.py:152
  9.9 42.7 %copy-start.10 = (s32[128]{0:T(128)S(1)}, s32[128]{0:T(128)}, u32[]{:S(2)}) copy-start(s32[128]{0:T(128)} %param.8) | copy-start | bytes 1540
  179.5 57.9 %all-to-all-start = ((bf16[32,1,128,128]{3,2,1,0:T(8,128)(2,1)}), bf16[32,1,128,128]{3,2,1,0:T(8,128)(2,1)S(1)}, u32[]{:S(2)}, u32[]{:S(2)}) async-start(bf16[32,1,128,128]{3,2,1,0:T(8,128)(2,1)} %constant_dynamic-update-slice_fusion), calls=%async_computation | async-start | bytes 2097152 | tf_op jit(solution)/shard_map/all_to_all | solution.py:128
  191.9 163.8 %all-gather.8.cloned.1.call-start = ((), (), s32[]{:S(2)}) async-start(), calls=%async_computation.2 | async-start | bytes 9437184 | tf_op jit(solution)/shard_map/all_gather | solution.py:186
  237.6 1.5 copy-start.9
  241.0 25.2 %collective-permute-start = (bf16[128,4096]{1,0:T(8,128)(2,1)S(1)}, bf16[128,4096]{1,0:T(8,128)(2,1)}, u32[]{:S(2)}, u32[]{:S(2)}) collective-permute-start(bf16[128,4096]{1,0:T(8,128)(2,1)S(1)} %fusion.15), channel_id=1, source_target_pairs={{0,1},{1,0},{2,3},{3,2},{4,5},{5,4},{6,7},{7,6},{8,9},{9,8},{10,11... | collective-permute-start | bytes 3145736 | tf_op jit(solution)/shard_map/ppermute | solution.py:21
  269.2 1.7 copy-start.1
  269.2 1.9 copy-start.11
  270.9 47.0 %collective-permute-start.1 = (bf16[256,4096]{1,0:T(8,128)(2,1)}, bf16[256,4096]{1,0:T(8,128)(2,1)}, u32[]{:S(2)}, u32[]{:S(2)}) collective-permute-start(bf16[256,4096]{1,0:T(8,128)(2,1)} %pad_maximum_fusion), channel_id=1, source_target_pairs={{0,2},{2,0},{1,3},{3,1},{4,6},{6,4},{5,7},{7,5},{8,10},{10,8},{9,1... | collective-permute-start | bytes 6291464 | tf_op jit(solution)/shard_map/ppermute | solution.py:21
  333.6 1.6 copy-start.4
  338.0 1.0 copy-start.5
  339.8 2.4 copy-start.6
  343.0 1.2 copy-start.2
  343.0 1.5 copy-start.3
  344.6 1.4 copy-start.7
  345.9 5.7 %copy-start.8 = (bf16[512,1,256]{0,2,1:T(8,128)(2,1)S(1)}, bf16[512,1,256]{0,2,1:T(8,128)(2,1)}, u32[]{:S(2)}) copy-start(bf16[512,1,256]{0,2,1:T(8,128)(2,1)} %copy.31) | copy-start | bytes 786436
  364.4 45.9 %collective-permute-start.2 = (bf16[256,4096]{1,0:T(8,128)(2,1)S(1)}, bf16[256,4096]{1,0:T(8,128)(2,1)S(1)}, u32[]{:S(2)}, u32[]{:S(2)}) collective-permute-start(bf16[256,4096]{1,0:T(8,128)(2,1)S(1)} %select_convert_fusion), channel_id=1, source_target_pairs={{0,2},{2,0},{1,3},{3,1},{4,6},{6,4},{5,7},{7,5},{8,10},{10,8},{9,1... | collective-permute-start | bytes 6291464 | tf_op jit(solution)/shard_map/ppermute | solution.py:21
  411.5 1.3 copy-start
  413.9 22.7 %collective-permute-start.3 = (bf16[128,4096]{1,0:T(8,128)(2,1)}, bf16[128,4096]{1,0:T(8,128)(2,1)S(1)}, u32[]{:S(2)}, u32[]{:S(2)}) collective-permute-start(bf16[128,4096]{1,0:T(8,128)(2,1)} %select_convert_fusion.2), channel_id=1, source_target_pairs={{0,1},{1,0},{2,3},{3,2},{4,5},{5,4},{6,7},{7,6},{8,9},{9,8},{10,11... | collective-permute-start | bytes 3145736 | tf_op jit(solution)/shard_map/ppermute | solution.py:21
Sparse Core Ops, SparseCore 0:
  10.0 114.7 all-gather.5
  194.4 90.8 all-gather.7
